TPU v7x, 256 devices: a whole 4x4x8 slice. The times are simulated.
256 devices in a mesh: role: 2 (over core), wide: 8 (over x_hi, y), tp: 16 (over z, x_lo).
Axes of the slice: x: 4 (x_hi: 2, x_lo: 2; x = x_hi * 2 + x_lo), y: 4, z: 8, core: 2. Of those that a mesh axis runs over, the one named last changes fastest.
Arguments:
- normed: bfloat16 [4096, 4096], P('wide', ('role', 'tp')), may hold values from -0.29882812 to 0.29882812
- queries: bfloat16 [4096, 4096], P('wide', 'tp'), may hold values from -4 to 4
- keys: bfloat16 [4096, 1024], P('wide'), may hold values from -4 to 4
- values: bfloat16 [4096, 1024], P('wide'), may hold values from -6 to 6
- attn_out: bfloat16 [4096, 4096], P('wide', 'tp'), may hold values from -0.29882812 to 0.29882812
- row_logsumexp: float32 [32, 4096], P('tp'), as said below
- out_grad: bfloat16 [4096, 4096], P('wide', ('role', 'tp')), may hold values from -6 to 6
- out_weight: bfloat16 [4096, 4096], P('tp'), may hold values from -0.09375 to 0.09375
- qkv_weight: bfloat16 [4096, 6144], P(('role', 'tp')), may hold values from -0.09375 to 0.09375
- documents: int32 [4096], replicated, may hold values from 0 to 2, as said below
- tasks: int32 [8, 16, 2], replicated, may hold values from -1 to 15, as said below
Outputs:
- normed_grad: bfloat16 [4096, 4096], P('wide', ('role', 'tp'))
- out_weight_grad: bfloat16 [4096, 4096], P('tp', ('role', 'wide'))
- qkv_weight_grad: bfloat16 [4096, 6144], P(('role', 'tp'), 'wide')
Inputs may be any that keep to these rules, and one draw needn't show every extreme that they name: `documents`: document numbers never fall along the tokens, and every number from 0 to 2 is used. `tasks`: row s lists in its first slots the query blocks of server s, in [s, j, 0], followed by slots holding -1 in both places; every query block from 0 to 15 stands in exactly one slot of the table; [s, j, 1] is the block holding the first token of the document of the query block's first token. row_logsumexp[h, i] is the logarithm of the sum, over the tokens j that token i may attend, of exp(scores[h, i, j]) as computed from queries and keys.
All inputs are finite; a program needn't handle non-finite values.
Results may differ from a plain program's by a relative error of at most 0.018.
Values may be sent and summed in bfloat16 or wider, within the bound.
A program may use at most 128 MiB of HBM per device.

v0:
```python
import jax
import jax.numpy as jnp
from jax import lax
from jax.sharding import PartitionSpec as P

D = 4096
QUERY_HEADS = 32
KEY_VALUE_HEADS = 8
HEAD_SIZE = 128


def cut_along(shard, dim, length):
    before, after = (shard.shape[:dim], shard.shape[dim + 1 :])
    return jnp.moveaxis(shard.reshape(*before, length, -1, *after), dim, 0)


def sum_at_owner(shard, axis, dim):
    tiles = cut_along(shard, dim, lax.axis_size(axis))
    arrived = lax.all_to_all(tiles, axis, split_axis=0, concat_axis=0, tiled=True)
    return arrived.astype(jnp.float32).sum(axis=0)


def in_one_piece(arrays, axis, dim, along):
    both = jnp.concatenate(arrays, axis=along)
    out, at, done = (lax.all_gather(both, axis, axis=dim, tiled=True), 0, [])
    for a in arrays:
        done.append(lax.slice_in_dim(out, at, at + a.shape[along], axis=along))
        at += a.shape[along]
    return tuple(done)


def local(
    normed,
    queries,
    keys,
    values,
    attn_out,
    row_logsumexp,
    out_grad,
    out_weight,
    qkv_weight,
    documents,
    tasks,
):
    role_pos = lax.axis_index("role")
    is_worker = role_pos == 0
    wide_count = lax.axis_size("wide")
    wide_pos = lax.axis_index("wide")
    tp_pos = lax.axis_index("tp")
    local_rows = normed.shape[0]
    row_halves = local_rows // 2
    head_count = queries.shape[1] // HEAD_SIZE
    pair_count = head_count // 2
    kv_count = max(1, head_count // 4)
    score_scale = HEAD_SIZE ** (-0.5)
    total_rows = wide_count * local_rows
    block_count = tasks.shape[1]
    full_grad = lax.all_gather(out_grad, ("role", "tp"), axis=1, tiled=True)
    grad_half = lax.dynamic_slice_in_dim(full_grad, role_pos * (D // 2), D // 2, 1)
    out_part = lax.dot_general(
        attn_out, grad_half, (((0,), (0,)), ((), ())), preferred_element_type=jnp.float32
    )
    out_sum = sum_at_owner(out_part.astype(jnp.bfloat16), "wide", 1)

    def worker_side():
        return lax.dot_general(
            full_grad, out_weight, (((1,), (1,)), ((), ())), preferred_element_type=jnp.float32
        ).astype(jnp.bfloat16)

    def server_side():
        return queries

    first_piece = lax.cond(is_worker, worker_side, server_side)
    kv_start = tp_pos * head_count // 4 * HEAD_SIZE
    key_cols = lax.dynamic_slice_in_dim(keys, kv_start, kv_count * HEAD_SIZE, 1)
    value_cols = lax.dynamic_slice_in_dim(values, kv_start, kv_count * HEAD_SIZE, 1)
    kv_piece = jnp.where(is_worker, key_cols, value_cols)
    out_piece = lax.dynamic_slice_in_dim(
        attn_out, role_pos * pair_count * HEAD_SIZE, pair_count * HEAD_SIZE, 1
    )
    gathered = in_one_piece((first_piece, kv_piece, out_piece), ("role", "wide"), 0, 1)
    grad_all = gathered[0][:total_rows]
    query_all = gathered[0][total_rows:]
    key_all = gathered[1][:total_rows]
    value_all = gathered[1][total_rows:]
    output_all = gathered[2].reshape(2, total_rows, pair_count, HEAD_SIZE)
    delta_all = jnp.einsum(
        "irpd,ripd->rpi",
        grad_all.reshape(total_rows, 2, pair_count, HEAD_SIZE),
        output_all,
        preferred_element_type=jnp.float32,
    ).reshape(pair_count, 2, total_rows)
    lse_all = row_logsumexp.reshape(pair_count, 2, total_rows)

    def tile(block_q, block_k, query_grad, kv_acc):
        offsets = jnp.arange(row_halves, dtype=jnp.int32)
        query_pos = block_q * row_halves + offsets
        key_pos = block_k * row_halves + offsets
        query_rows = lax.dynamic_slice_in_dim(
            query_all, block_q * row_halves, row_halves, 0
        ).reshape(row_halves, pair_count, 2, HEAD_SIZE)
        grad_rows = lax.dynamic_slice_in_dim(grad_all, block_q * row_halves, row_halves, 0).reshape(
            row_halves, pair_count, 2, HEAD_SIZE
        )
        key_rows = lax.dynamic_slice_in_dim(key_all, block_k * row_halves, row_halves, 0).reshape(
            row_halves, kv_count, HEAD_SIZE
        )
        value_rows = lax.dynamic_slice_in_dim(
            value_all, block_k * row_halves, row_halves, 0
        ).reshape(row_halves, kv_count, HEAD_SIZE)
        lse_rows = lax.dynamic_slice_in_dim(lse_all, block_q * row_halves, row_halves, 2)
        delta_rows = lax.dynamic_slice_in_dim(delta_all, block_q * row_halves, row_halves, 2)
        query_docs = lax.dynamic_slice_in_dim(documents, block_q * row_halves, row_halves, 0)
        key_docs = lax.dynamic_slice_in_dim(documents, block_k * row_halves, row_halves, 0)
        allowed = (query_docs[:, None] == key_docs[None, :]) & (
            key_pos[None, :] <= query_pos[:, None]
        )
        scores = (
            jnp.einsum("qphd,cpd->phqc", query_rows, key_rows, preferred_element_type=jnp.float32)
            * score_scale
        )
        probs = jnp.exp(jnp.where(allowed, scores - lse_rows[..., None], -jnp.inf))
        probs_low = probs.astype(jnp.bfloat16)
        value_grad = jnp.einsum(
            "phqc,qphd->cpd", probs_low, grad_rows, preferred_element_type=jnp.float32
        )
        prob_grad = jnp.einsum(
            "qphd,cpd->phqc", grad_rows, value_rows, preferred_element_type=jnp.float32
        )
        score_grad = (probs * (prob_grad - delta_rows[..., None]) * score_scale).astype(
            jnp.bfloat16
        )
        query_tile = jnp.einsum(
            "phqc,cpd->qphd", score_grad, key_rows, preferred_element_type=jnp.float32
        )
        query_grad = query_grad + query_tile.reshape(row_halves, head_count * HEAD_SIZE)
        key_grad = jnp.einsum(
            "phqc,qphd->cpd", score_grad, query_rows, preferred_element_type=jnp.float32
        )
        tile_kv = jnp.concatenate([key_grad, value_grad], axis=2).reshape(
            row_halves, pair_count * 2 * HEAD_SIZE
        )
        target = block_k % 2 * wide_count + block_k // 2
        current = lax.dynamic_index_in_dim(kv_acc, target, 0, keepdims=False)
        kv_acc = lax.dynamic_update_index_in_dim(kv_acc, current + tile_kv, target, 0)
        return (query_grad, kv_acc)

    def empty_side():
        return (
            jnp.zeros((block_count, row_halves, head_count * HEAD_SIZE), jnp.float32),
            jnp.zeros((block_count, row_halves, pair_count * 2 * HEAD_SIZE), jnp.float32),
        )

    def attend_side():
        own_row = lax.dynamic_index_in_dim(tasks, wide_pos, 0, keepdims=False)

        def slot_turn(number, carry):
            query_acc, kv_acc = carry
            block_q = own_row[number, 0]
            valid = block_q >= 0
            safe_q = jnp.maximum(block_q, 0)
            upper = jnp.where(valid, safe_q + 1, 0)
            lower = jnp.where(valid, own_row[number, 1], 0)

            def key_turn(block_k, inner):
                return tile(safe_q, block_k, inner[0], inner[1])

            start = jnp.zeros((row_halves, head_count * HEAD_SIZE), jnp.float32)
            query_grad, kv_acc = lax.fori_loop(lower, upper, key_turn, (start, kv_acc))
            target = safe_q % 2 * wide_count + safe_q // 2
            current = lax.dynamic_index_in_dim(query_acc, target, 0, keepdims=False)
            query_acc = lax.dynamic_update_index_in_dim(query_acc, current + query_grad, target, 0)
            return (query_acc, kv_acc)

        return lax.fori_loop(0, block_count, slot_turn, empty_side())

    query_acc, kv_acc = lax.cond(is_worker, empty_side, attend_side)
    kv_flat = kv_acc.reshape(block_count * row_halves, pair_count * 2 * HEAD_SIZE)
    kv_sum = sum_at_owner(kv_flat.astype(jnp.bfloat16), ("role", "wide"), 0)
    arrived = lax.all_to_all(
        query_acc.astype(jnp.bfloat16), ("role", "wide"), split_axis=0, concat_axis=0, tiled=True
    )
    query_piece = jnp.sum(arrived.astype(jnp.float32), axis=0).astype(jnp.bfloat16)
    head_q, key_value_head = in_one_piece(
        (query_piece, kv_sum.astype(jnp.bfloat16)), ("role", "tp"), 1, 0
    )
    query_grads = head_q.reshape(row_halves, 2, QUERY_HEADS * HEAD_SIZE)
    grouped_queries = jnp.sum(
        key_value_head.reshape(row_halves, 2, KEY_VALUE_HEADS, 2, 2 * HEAD_SIZE).astype(
            jnp.float32
        ),
        axis=3,
    ).astype(jnp.bfloat16)
    key_gradients = grouped_queries[..., :HEAD_SIZE].reshape(
        row_halves, 2, KEY_VALUE_HEADS * HEAD_SIZE
    )
    value_gradients = grouped_queries[..., HEAD_SIZE:].reshape(
        row_halves, 2, KEY_VALUE_HEADS * HEAD_SIZE
    )
    qkv_grads = jnp.concatenate([query_grads, key_gradients, value_gradients], axis=2)
    normed_grad = jnp.einsum(
        "irc,nc->rin", qkv_grads, qkv_weight, preferred_element_type=jnp.float32
    )
    normed_grad = normed_grad.reshape(local_rows, qkv_weight.shape[0]).astype(jnp.bfloat16)
    qkv_part = jnp.einsum(
        "rin,irc->nc",
        normed.reshape(2, row_halves, normed.shape[1]),
        qkv_grads,
        preferred_element_type=jnp.float32,
    )
    qkv_sum = sum_at_owner(qkv_part.astype(jnp.bfloat16), "wide", 1)
    return (normed_grad, out_sum.astype(jnp.bfloat16), qkv_sum.astype(jnp.bfloat16))


def solution(mesh):
    in_specs = (
        P("wide", ("role", "tp")),
        P("wide", "tp"),
        P("wide", None),
        P("wide", None),
        P("wide", "tp"),
        P("tp", None),
        P("wide", ("role", "tp")),
        P("tp", None),
        P(("role", "tp"), None),
        P(),
        P(),
    )
    out_specs = (P("wide", ("role", "tp")), P("tp", ("role", "wide")), P(("role", "tp"), "wide"))
    return jax.shard_map(local, mesh=mesh, in_specs=in_specs, out_specs=out_specs, check_vma=False)
```

profile of v0, /device:TPU:1, one launch (start us, length us, event | category | flops | bytes accessed | tf_op | source)
XLA Modules:
  0.0 605.2 jit_solution(3537214650441579339)
XLA Ops:
  10.3 75.8 %all-gather.4.cloned.1.call-done = bf16[512,4096]{1,0:T(8,128)(2,1)} async-done(((bf16[512,128]{1,0:T(8,128)(2,1)}), bf16[512,4096]{1,0:T(8,128)(2,1)}) %all-gather.4.cloned.1.call-update) | async-done | bytes 4194320 | tf_op jit(solution)/shard_map/all_gather | solution.py:58
  88.1 83.6 %all-gather.6.cloned.1.call-done = bf16[8192,512]{0,1:T(8,128)(2,1)} async-done(((bf16[512,512]{0,1:T(8,128)(2,1)}), bf16[8192,512]{0,1:T(8,128)(2,1)}) %all-gather.6.cloned.1.call-update) | async-done | bytes 8388624 | tf_op jit(solution)/shard_map/all_gather | solution.py:25
  174.9 4.1 convert.5
  179.0 214.2 %conditional.3 = (f32[16,256,256]{1,2,0:T(8,128)}, f32[16,256,256]{1,2,0:T(8,128)}) conditional(s32[]{:T(128)} %convert_element_type.57, (s32[]{:T(128)}, s32[8,16,2]{1,2,0:T(2,128)}, s32[4096]{0:T(1024)}, bf16[8192,512]{0,1:T(8,128)(2,1)}, f32[2,4096]{1,0:T(2,128)}, /*index=5*/bf16[4096,256]{0,1:T(8,128)(2,1)}, f32[2,4096,128]{1,2,0:T(8,128)}, ...), branch_computations={%region_2.7_spmd.clone, %region_7.8_spmd} | conditional | flops 172417568 | bytes 72474416 | solution.py:177
  182.8 4.5 reshape.193
  187.3 6.8 %fusion.23 = f32[2,4096]{1,0:T(2,128)S(1)} fusion(bf16[2,4096,128]{1,0,2:T(2,128)(2,1)} %reshape.193, f32[2,4096,128]{1,2,0:T(8,128)} %get-tuple-element.631), kind=kLoop, calls=%fused_computation.43 | loop fusion | flops 3137536 | bytes 6324224 | tf_op jit(solution)/shard_map/irpd,ripd->rpi/dot_general | solution.py:87
  197.3 11.6 %copy.83 = bf16[8192,512]{1,0:T(8,128)(2,1)} copy(bf16[8192,512]{0,1:T(8,128)(2,1)} %get-tuple-element.632) | data formatting | bytes 16777216 | tf_op jit(solution)/shard_map
  210.2 11.6 %copy.82 = bf16[8192,512]{1,0:T(8,128)(2,1)} copy(bf16[8192,512]{0,1:T(8,128)(2,1)} %get-tuple-element.632) | data formatting | bytes 16777216 | tf_op jit(solution)/shard_map
  229.0 164.3 %while.56 = (s32[]{:T(128)}, f32[16,256,256]{1,2,0:T(8,128)}, f32[16,256,256]{1,2,0:T(8,128)}, s32[16,2]{0,1:T(2,128)S(1)}, s32[4096]{0:T(1024)}, /*index=5*/bf1...) while((s32[]{:T(128)}, f32[16,256,256]{1,2,0:T(8,128)}, ...), condition=%wide.region_6.6_spmd, body=%wide.region_3.5_spmd.sunk | while | flops 169280032 | bytes 7429371 | solution.py:175
  235.0 55.2 %while.57 = (s32[]{:T(128)}, f32[256,256]{0,1:T(8,128)S(1)}, f32[16,256,256]{1,2,0:T(8,128)}, s32[]{:T(128)}, bf16[4096,128]{1,0:T(8,128)(2,1)}, /*index=5*/s32[...) while((s32[]{:T(128)}, f32[256,256]{0,1:T(8,128)S(1)}, ...), condition=%wide.region_5.4_spmd, body=%wide.region_4.3_spmd.sunk | while | flops 169214464 | bytes 5321220 | solution.py:169
  393.2 3.8 convert_element_type.58
  397.0 4.3 all-to-all-start
  401.4 3.8 convert_element_type.59
  405.1 23.5 %all-to-all-done = bf16[16,256,256]{1,2,0:T(8,128)(2,1)} async-done(((bf16[16,256,256]{1,2,0:T(8,128)(2,1)}), bf16[16,256,256]{1,2,0:T(8,128)(2,1)}, u32[]{:S(2)}, u32[]{:S(2)}) %all-to-all-start) | async-done | bytes 2097184 | tf_op jit(solution)/shard_map/all_to_all | solution.py:180
  428.6 4.5 all-to-all-start.1
  435.2 26.9 %all-to-all-done.1 = bf16[16,256,256]{1,2,0:T(8,128)(2,1)} async-done(((bf16[16,256,256]{1,2,0:T(8,128)(2,1)}), bf16[16,256,256]{1,2,0:T(8,128)(2,1)}, u32[]{:S(2)}, u32[]{:S(2)}) %all-to-all-start.1) | async-done | bytes 2097184 | tf_op jit(solution)/shard_map/all_to_all | solution.py:19
  471.8 67.4 %all-gather.8.cloned.1.call-done = bf16[512,8192]{0,1:T(8,128)(2,1)} async-done(((bf16[512,256]{0,1:T(8,128)(2,1)}), bf16[512,8192]{0,1:T(8,128)(2,1)}) %all-gather.8.cloned.1.call-update) | async-done | bytes 8388624 | tf_op jit(solution)/shard_map/all_gather | solution.py:25
  539.2 5.7 fusion.34
  544.9 6.4 %copy.60 = bf16[256,2,4096]{2,0,1:T(8,128)(2,1)} copy(bf16[256,2,4096]{0,2,1:T(8,128)(2,1)} %bitcast.194) | data formatting | bytes 8388608 | tf_op jit(solution)/shard_map/reshape | solution.py:187
  551.3 4.9 reduce_sum.62
  563.8 5.4 fusion.24
  570.2 6.8 %all-to-all-start.3 = ((bf16[8,128,768]{1,2,0:T(8,128)(2,1)}), bf16[8,128,768]{1,2,0:T(8,128)(2,1)S(1)}, u32[]{:S(2)}, u32[]{:S(2)}) async-start(bf16[8,128,768]{1,2,0:T(8,128)(2,1)} %bitcast.198), calls=%async_computation.3 | async-start | bytes 3145728 | tf_op jit(solution)/shard_map/all_to_all | solution.py:19
  579.1 6.1 %fusion.28 = bf16[256,2,128]{2,0,1:T(8,128)(2,1)} fusion(bf16[128,6144]{1,0:T(8,128)(2,1)S(1)} %copy-done, bf16[256,2,1024]{2,0,1:T(8,128)(2,1)} %copy.78, bf16[256,2,1024]{2,0,1:T(8,128)(2,1)} %copy.77, bf16[256,2,4096]{2,0,1:T(8,128)(2,1)} %copy.60), kind=kOutput, calls=%fused_computation.52 | convolution fusion | flops 824246272 | bytes 7995392 | tf_op jit(solution)/shard_map/irc,nc->rin/dot_general | solution.py:201
  585.2 12.4 %all-to-all-done.3 = bf16[8,128,768]{1,2,0:T(8,128)(2,1)S(1)} async-done(((bf16[8,128,768]{1,2,0:T(8,128)(2,1)}), bf16[8,128,768]{1,2,0:T(8,128)(2,1)S(1)}, u32[]{:S(2)}, u32[]{:S(2)}) %all-to-all-start.3) | async-done | bytes 1572896 | tf_op jit(solution)/shard_map/all_to_all | solution.py:19
  (271 shorter events, 180.4 us)
Async XLA Ops:
  7.2 572.0 %copy-start = (bf16[128,6144]{1,0:T(8,128)(2,1)S(1)}, bf16[128,6144]{1,0:T(8,128)(2,1)}, u32[]{:S(2)}) copy-start(bf16[128,6144]{1,0:T(8,128)(2,1)} %param.27) | copy-start | bytes 4718596
  7.2 78.9 %all-gather.4.cloned.1.call-start = ((), (), s32[]{:S(2)}) async-start(), calls=%async_computation.4 | async-start | bytes 4325376 | tf_op jit(solution)/shard_map/all_gather | solution.py:58
  7.9 163.8 %all-gather.6.cloned.1.call-start = ((), (), s32[]{:S(2)}) async-start(), calls=%async_computation.5 | async-start | bytes 8912896 | tf_op jit(solution)/shard_map/all_gather | solution.py:25
  397.0 31.6 %all-to-all-start = ((bf16[16,256,256]{1,2,0:T(8,128)(2,1)}), bf16[16,256,256]{1,2,0:T(8,128)(2,1)}, u32[]{:S(2)}, u32[]{:S(2)}) async-start(bf16[16,256,256]{1,2,0:T(8,128)(2,1)} %convert_element_type.58), calls=%async_computation | async-start | bytes 4194304 | tf_op jit(solution)/shard_map/all_to_all | solution.py:180
  405.1 59.6 %copy-start.2 = (bf16[512,256]{1,0:T(8,128)(2,1)S(1)}, bf16[512,256]{1,0:T(8,128)(2,1)}, u32[]{:S(2)}) copy-start(bf16[512,256]{1,0:T(8,128)(2,1)} %param.23) | copy-start | bytes 786436
  428.6 33.5 %all-to-all-start.1 = ((bf16[16,256,256]{1,2,0:T(8,128)(2,1)}), bf16[16,256,256]{1,2,0:T(8,128)(2,1)}, u32[]{:S(2)}, u32[]{:S(2)}) async-start(bf16[16,256,256]{1,2,0:T(8,128)(2,1)} %convert_element_type.59), calls=%async_computation.1 | async-start | bytes 4194304 | tf_op jit(solution)/shard_map/all_to_all | solution.py:19
  433.1 106.0 %all-gather.8.cloned.1.call-start = ((), (), s32[]{:S(2)}) async-start(), calls=%async_computation.6 | async-start | bytes 8650752 | tf_op jit(solution)/shard_map/all_gather | solution.py:25
  468.1 101.1 %all-to-all-start.2 = ((bf16[8,256,256]{1,2,0:T(8,128)(2,1)}), bf16[8,256,256]{1,2,0:T(8,128)(2,1)S(1)}, u32[]{:S(2)}, u32[]{:S(2)}) async-start(bf16[8,256,256]{1,2,0:T(8,128)(2,1)} %bitcast.199), calls=%async_computation.2 | async-start | bytes 2097152 | tf_op jit(solution)/shard_map/all_to_all | solution.py:19
  556.1 7.7 %copy-start.3 = (bf16[512,128]{1,0:T(8,128)(2,1)S(1)}, bf16[512,128]{1,0:T(8,128)(2,1)}, u32[]{:S(2)}) copy-start(bf16[512,128]{1,0:T(8,128)(2,1)} %param.19) | copy-start | bytes 393220
  569.2 1.0 copy-start.1
  570.2 27.3 %all-to-all-start.3 = ((bf16[8,128,768]{1,2,0:T(8,128)(2,1)}), bf16[8,128,768]{1,2,0:T(8,128)(2,1)S(1)}, u32[]{:S(2)}, u32[]{:S(2)}) async-start(bf16[8,128,768]{1,2,0:T(8,128)(2,1)} %bitcast.198), calls=%async_computation.3 | async-start | bytes 3145728 | tf_op jit(solution)/shard_map/all_to_all | solution.py:19
Sparse Core Ops, SparseCore 0:
  9.8 76.3 all-gather.3
  88.7 83.0 all-gather.5
  464.9 74.2 all-gather.7
where the time goes:
time: 611 us; the launch traced here: 605 us
  waiting for transfers between devices  290 us (47%)
  local copies, waits for them, and re-layouts  145 us (24%)
  other arithmetic  61.1 us (10%)
  matrix products  42.8 us (7%)
  loops' own time  32.5 us (5%)
  starting transfers between devices  19.6 us (3%)
  between operations  13.9 us (2%)
    all_gather x2, waiting for transfers between devices, in_one_piece(): out, at, done = (lax.all_gather(both, axis, axis=dim, tiled=True), 0, [])  151 us
    all_gather x1, waiting for transfers between devices, local(): full_grad = lax.all_gather(out_grad, ('role', 'tp'), axis=1, tiled=True)  75.8 us
    all_to_all x3, waiting for transfers between devices, sum_at_owner(): lax.all_to_all(tiles, axis, split_axis=0, concat_axis=0, tiled=True)  39.3 us
    another operation x21, local copies, waits for them, and re-layouts  32.8 us
    another operation x1, loops' own time, attend_side(): return lax.fori_loop(0, block_count, slot_turn, empty_side())  31.7 us
    all_to_all x1, waiting for transfers between devices, local(): lax.all_to_all(query_acc.astype(jnp.bfloat16), ('role', 'wide'), split_ax...  23.5 us
    dynamic_update_slice x10, other arithmetic, tile(): lax.dynamic_update_index_in_dim(kv_acc, current + tile_kv, target, 0)  17 us
    dynamic_slice x16, local copies, waits for them, and re-layouts, tile(): lax.dynamic_slice_in_dim(grad_all, block_q * row_halves, row_halves, 0)  15.8 us
  transfers between devices with their start and end apart: 7, of which 6 were waited for; matrix products, arithmetic and copies ran while one was open for 8% of the time, Pallas kernels for 0%

commit v1 on v0

--- a/solution.py
+++ b/solution.py
@@ -55,7 +55,10 @@
     score_scale = HEAD_SIZE ** (-0.5)
     total_rows = wide_count * local_rows
     block_count = tasks.shape[1]
-    full_grad = lax.all_gather(out_grad, ("role", "tp"), axis=1, tiled=True)
+    full_grad = jnp.concatenate(
+        lax.all_to_all(jnp.stack([out_grad] * lax.axis_size(("role", "tp"))), ("role", "tp"), 0, 0),
+        axis=1,
+    )
     grad_half = lax.dynamic_slice_in_dim(full_grad, role_pos * (D // 2), D // 2, 1)
     out_part = lax.dot_general(
         attn_out, grad_half, (((0,), (0,)), ((), ())), preferred_element_type=jnp.float32

time: 611 us -> 650 us (1.064)
  waiting for transfers between devices: 290 us -> 310 us
  starting transfers between devices: 19.6 us -> 30.8 us
  local copies, waits for them, and re-layouts: 145 us -> 153 us
    all_to_all x0 -> x1, waiting for transfers between devices: none -> 95.8 us  [local(): lax.all_to_all(jnp.stack([out_grad] * lax.axis_size(('role', 'tp'))), ('r...]
    all_gather x1 -> x0, waiting for transfers between devices: 75.8 us -> none  [local(): full_grad = lax.all_gather(out_grad, ('role', 'tp'), axis=1, tiled=True)]
    all_to_all x0 -> x1, starting transfers between devices: none -> 11.2 us  [local(): lax.all_to_all(jnp.stack([out_grad] * lax.axis_size(('role', 'tp'))), ('r...]
    another operation x21 -> x22, local copies, waits for them, and re-layouts: 32.8 us -> 36.6 us
where the time goes in v1:
time: 650 us; the launch traced here: 644 us
  waiting for transfers between devices  310 us (48%)
  local copies, waits for them, and re-layouts  153 us (24%)
  other arithmetic  61.4 us (9%)
  matrix products  42.7 us (7%)
  loops' own time  31.4 us (5%)
  starting transfers between devices  30.8 us (5%)
  between operations  14.2 us (2%)
    all_gather x2, waiting for transfers between devices, in_one_piece(): out, at, done = (lax.all_gather(both, axis, axis=dim, tiled=True), 0, [])  152 us
    all_to_all x1, waiting for transfers between devices, local(): lax.all_to_all(jnp.stack([out_grad] * lax.axis_size(('role', 'tp'))), ('r...  95.8 us
    all_to_all x3, waiting for transfers between devices, sum_at_owner(): lax.all_to_all(tiles, axis, split_axis=0, concat_axis=0, tiled=True)  39.4 us
    another operation x21, local copies, waits for them, and re-layouts  32.7 us
    another operation x1, loops' own time, attend_side(): return lax.fori_loop(0, block_count, slot_turn, empty_side())  30.6 us
    all_to_all x1, waiting for transfers between devices, local(): lax.all_to_all(query_acc.astype(jnp.bfloat16), ('role', 'wide'), split_ax...  23.4 us
    dynamic_update_slice x10, other arithmetic, tile(): lax.dynamic_update_index_in_dim(kv_acc, current + tile_kv, target, 0)  17 us
    dynamic_slice x16, local copies, waits for them, and re-layouts, tile(): lax.dynamic_slice_in_dim(grad_all, block_q * row_halves, row_halves, 0)  15.8 us
  transfers between devices with their start and end apart: 7, of which 6 were waited for; matrix products, arithmetic and copies ran while one was open for 8% of the time, Pallas kernels for 0%

profile of v1, /device:TPU:1, one launch (start us, length us, event | category | flops | bytes accessed | tf_op | source)
XLA Modules:
  0.0 644.3 jit_solution(11085544233110148538)
XLA Ops:
  11.1 11.2 %all-to-all-start = ((bf16[32,512,128]{2,1,0:T(8,128)(2,1)}), bf16[32,512,128]{2,1,0:T(8,128)(2,1)}, u32[]{:S(2)}, u32[]{:S(2)}) async-start(bf16[32,512,128]{2,1,0:T(8,128)(2,1)} %stack.2), calls=%async_computation | async-start | bytes 8388608 | tf_op jit(solution)/shard_map/all_to_all | solution.py:59
  23.9 95.8 %all-to-all-done = bf16[32,512,128]{2,1,0:T(8,128)(2,1)} async-done(((bf16[32,512,128]{2,1,0:T(8,128)(2,1)}), bf16[32,512,128]{2,1,0:T(8,128)(2,1)}, u32[]{:S(2)}, u32[]{:S(2)}) %all-to-all-start) | async-done | bytes 4194336 | tf_op jit(solution)/shard_map/all_to_all | solution.py:59
  119.7 6.5 %copy.70 = bf16[32,512,128]{1,2,0:T(8,128)(2,1)} copy(bf16[32,512,128]{2,1,0:T(8,128)(2,1)} %all-to-all-done) | data formatting | bytes 8388608 | tf_op jit(solution)/shard_map/all_to_all | solution.py:59
  127.2 84.4 %all-gather.3.cloned.1.call-done = bf16[8192,512]{0,1:T(8,128)(2,1)} async-done(((bf16[512,512]{0,1:T(8,128)(2,1)}), bf16[8192,512]{0,1:T(8,128)(2,1)}) %all-gather.3.cloned.1.call-update) | async-done | bytes 8388624 | tf_op jit(solution)/shard_map/all_gather | solution.py:25
  214.8 4.1 convert.5
  218.9 213.0 %conditional.3 = (f32[16,256,256]{1,2,0:T(8,128)}, f32[16,256,256]{1,2,0:T(8,128)}) conditional(s32[]{:T(128)} %convert_element_type.57, (s32[]{:T(128)}, s32[8,16,2]{1,2,0:T(2,128)}, s32[4096]{0:T(1024)}, bf16[8192,512]{0,1:T(8,128)(2,1)}, f32[2,4096]{1,0:T(2,128)}, /*index=5*/bf16[4096,256]{0,1:T(8,128)(2,1)}, f32[2,4096,128]{1,2,0:T(8,128)}, ...), branch_computations={%region_2.7_spmd.clone, %region_7.8_spmd} | conditional | flops 172417568 | bytes 72474416 | solution.py:180
  222.7 4.5 reshape.203
  227.2 6.8 %fusion.23 = f32[2,4096]{1,0:T(2,128)S(1)} fusion(bf16[2,4096,128]{1,0,2:T(2,128)(2,1)} %reshape.203, f32[2,4096,128]{1,2,0:T(8,128)} %get-tuple-element.645), kind=kLoop, calls=%fused_computation.43 | loop fusion | flops 3137536 | bytes 6324224 | tf_op jit(solution)/shard_map/irpd,ripd->rpi/dot_general | solution.py:90
  237.2 11.5 %copy.104 = bf16[8192,512]{1,0:T(8,128)(2,1)} copy(bf16[8192,512]{0,1:T(8,128)(2,1)} %get-tuple-element.646) | data formatting | bytes 16777216 | tf_op jit(solution)/shard_map
  250.0 11.6 %copy.103 = bf16[8192,512]{1,0:T(8,128)(2,1)} copy(bf16[8192,512]{0,1:T(8,128)(2,1)} %get-tuple-element.646) | data formatting | bytes 16777216 | tf_op jit(solution)/shard_map
  268.7 163.2 %while.56 = (s32[]{:T(128)}, f32[16,256,256]{1,2,0:T(8,128)}, f32[16,256,256]{1,2,0:T(8,128)}, s32[16,2]{0,1:T(2,128)S(1)}, s32[4096]{0:T(1024)}, /*index=5*/bf1...) while((s32[]{:T(128)}, f32[16,256,256]{1,2,0:T(8,128)}, ...), condition=%wide.region_6.6_spmd, body=%wide.region_3.5_spmd.sunk | while | flops 169280032 | bytes 7429371 | solution.py:178
  274.6 55.2 %while.57 = (s32[]{:T(128)}, f32[256,256]{0,1:T(8,128)S(1)}, f32[16,256,256]{1,2,0:T(8,128)}, s32[]{:T(128)}, bf16[4096,128]{1,0:T(8,128)(2,1)}, /*index=5*/s32[...) while((s32[]{:T(128)}, f32[256,256]{0,1:T(8,128)S(1)}, ...), condition=%wide.region_5.4_spmd, body=%wide.region_4.3_spmd.sunk | while | flops 169214464 | bytes 5321220 | solution.py:172
  435.6 4.3 all-to-all-start.1
  443.8 23.4 %all-to-all-done.1 = bf16[16,256,256]{1,2,0:T(8,128)(2,1)} async-done(((bf16[16,256,256]{1,2,0:T(8,128)(2,1)}), bf16[16,256,256]{1,2,0:T(8,128)(2,1)}, u32[]{:S(2)}, u32[]{:S(2)}) %all-to-all-start.1) | async-done | bytes 2097184 | tf_op jit(solution)/shard_map/all_to_all | solution.py:183
  467.2 4.5 all-to-all-start.2
  473.6 27.1 %all-to-all-done.2 = bf16[16,256,256]{1,2,0:T(8,128)(2,1)} async-done(((bf16[16,256,256]{1,2,0:T(8,128)(2,1)}), bf16[16,256,256]{1,2,0:T(8,128)(2,1)}, u32[]{:S(2)}, u32[]{:S(2)}) %all-to-all-start.2) | async-done | bytes 2097184 | tf_op jit(solution)/shard_map/all_to_all | solution.py:19
  510.3 67.4 %all-gather.5.cloned.1.call-done = bf16[512,8192]{0,1:T(8,128)(2,1)} async-done(((bf16[512,256]{0,1:T(8,128)(2,1)}), bf16[512,8192]{0,1:T(8,128)(2,1)}) %all-gather.5.cloned.1.call-update) | async-done | bytes 8388624 | tf_op jit(solution)/shard_map/all_gather | solution.py:25
  577.7 5.7 fusion.34
  583.4 6.4 copy.80
  589.8 4.9 reduce_sum.62
  602.4 5.4 fusion.24
  608.8 6.9 %all-to-all-start.4 = ((bf16[8,128,768]{1,2,0:T(8,128)(2,1)}), bf16[8,128,768]{1,2,0:T(8,128)(2,1)S(1)}, u32[]{:S(2)}, u32[]{:S(2)}) async-start(bf16[8,128,768]{1,2,0:T(8,128)(2,1)} %bitcast.204), calls=%async_computation.4 | async-start | bytes 3145728 | tf_op jit(solution)/shard_map/all_to_all | solution.py:19
  617.9 6.1 fusion.28
  624.0 12.4 %all-to-all-done.4 = bf16[8,128,768]{1,2,0:T(8,128)(2,1)S(1)} async-done(((bf16[8,128,768]{1,2,0:T(8,128)(2,1)}), bf16[8,128,768]{1,2,0:T(8,128)(2,1)S(1)}, u32[]{:S(2)}, u32[]{:S(2)}) %all-to-all-start.4) | async-done | bytes 1572896 | tf_op jit(solution)/shard_map/all_to_all | solution.py:19
  (276 shorter events, 188.2 us)
Async XLA Ops:
  7.2 610.8 %copy-start = (bf16[128,6144]{1,0:T(8,128)(2,1)S(1)}, bf16[128,6144]{1,0:T(8,128)(2,1)}, u32[]{:S(2)}) copy-start(bf16[128,6144]{1,0:T(8,128)(2,1)} %param.27) | copy-start | bytes 4718596
  11.1 11.3 %copy-start.2 = (bf16[512,256]{1,0:T(8,128)(2,1)S(1)}, bf16[512,256]{1,0:T(8,128)(2,1)}, u32[]{:S(2)}) copy-start(bf16[512,256]{1,0:T(8,128)(2,1)} %param.23) | copy-start | bytes 786436
  11.1 108.6 %all-to-all-start = ((bf16[32,512,128]{2,1,0:T(8,128)(2,1)}), bf16[32,512,128]{2,1,0:T(8,128)(2,1)}, u32[]{:S(2)}, u32[]{:S(2)}) async-start(bf16[32,512,128]{2,1,0:T(8,128)(2,1)} %stack.2), calls=%async_computation | async-start | bytes 8388608 | tf_op jit(solution)/shard_map/all_to_all | solution.py:59
  22.4 189.2 %all-gather.3.cloned.1.call-start = ((), (), s32[]{:S(2)}) async-start(), calls=%async_computation.5 | async-start | bytes 8912896 | tf_op jit(solution)/shard_map/all_gather | solution.py:25
  23.9 102.3 %copy-start.4 = (bf16[512,256]{1,0:T(8,128)(2,1)S(1)}, bf16[512,256]{1,0:T(8,128)(2,1)}, u32[]{:S(2)}) copy-start(bf16[512,256]{1,0:T(8,128)(2,1)} %param.20) | copy-start | bytes 786436
  435.6 31.5 %all-to-all-start.1 = ((bf16[16,256,256]{1,2,0:T(8,128)(2,1)}), bf16[16,256,256]{1,2,0:T(8,128)(2,1)}, u32[]{:S(2)}, u32[]{:S(2)}) async-start(bf16[16,256,256]{1,2,0:T(8,128)(2,1)} %convert_element_type.58), calls=%async_computation.1 | async-start | bytes 4194304 | tf_op jit(solution)/shard_map/all_to_all | solution.py:183
  443.8 59.6 %copy-start.3 = (bf16[512,256]{1,0:T(8,128)(2,1)S(1)}, bf16[512,256]{1,0:T(8,128)(2,1)}, u32[]{:S(2)}) copy-start(bf16[512,256]{1,0:T(8,128)(2,1)} %param.23) | copy-start | bytes 786436
  467.2 33.5 %all-to-all-start.2 = ((bf16[16,256,256]{1,2,0:T(8,128)(2,1)}), bf16[16,256,256]{1,2,0:T(8,128)(2,1)}, u32[]{:S(2)}, u32[]{:S(2)}) async-start(bf16[16,256,256]{1,2,0:T(8,128)(2,1)} %convert_element_type.59), calls=%async_computation.2 | async-start | bytes 4194304 | tf_op jit(solution)/shard_map/all_to_all | solution.py:19
  471.7 106.0 %all-gather.5.cloned.1.call-start = ((), (), s32[]{:S(2)}) async-start(), calls=%async_computation.6 | async-start | bytes 8650752 | tf_op jit(solution)/shard_map/all_gather | solution.py:25
  506.6 101.2 %all-to-all-start.3 = ((bf16[8,256,256]{1,2,0:T(8,128)(2,1)}), bf16[8,256,256]{1,2,0:T(8,128)(2,1)S(1)}, u32[]{:S(2)}, u32[]{:S(2)}) async-start(bf16[8,256,256]{1,2,0:T(8,128)(2,1)} %bitcast.200), calls=%async_computation.3 | async-start | bytes 2097152 | tf_op jit(solution)/shard_map/all_to_all | solution.py:19
  594.7 7.7 %copy-start.5 = (bf16[512,128]{1,0:T(8,128)(2,1)S(1)}, bf16[512,128]{1,0:T(8,128)(2,1)}, u32[]{:S(2)}) copy-start(bf16[512,128]{1,0:T(8,128)(2,1)} %param.19) | copy-start | bytes 393220
  607.8 1.0 copy-start.1
  608.8 27.5 %all-to-all-start.4 = ((bf16[8,128,768]{1,2,0:T(8,128)(2,1)}), bf16[8,128,768]{1,2,0:T(8,128)(2,1)S(1)}, u32[]{:S(2)}, u32[]{:S(2)}) async-start(bf16[8,128,768]{1,2,0:T(8,128)(2,1)} %bitcast.204), calls=%async_computation.4 | async-start | bytes 3145728 | tf_op jit(solution)/shard_map/all_to_all | solution.py:19
Sparse Core Ops, SparseCore 0:
  127.4 84.1 all-gather.2
  503.4 74.2 all-gather.4
